TPU v7x, 32 devices: a whole 2x2x4 slice. The times are simulated.
32 devices in a mesh: adapter: 8 (over z, y), tensor: 4 (over x, core).
Axes of the slice: x: 2, y: 2, z: 4, core: 2. Of those that a mesh axis runs over, the one named last changes fastest.
Arguments:
- hidden: bfloat16 [256, 4096], P('adapter', 'tensor'), may hold values from -6 to 6
- request_adapter: int32 [256, 1], P('adapter'), may hold values from 0 to 15; in each aligned block of 32 rows (0 to 31, 32 to 63, ...) at most 2 rows name the same one
- adapter_table_row: int32 [16], replicated, may hold values from 0 to 15, each once
- query_base_weight: bfloat16 [4096, 4096], P(None, 'tensor'), may hold values from -0.09375 to 0.09375
- down_weight: bfloat16 [16, 4096, 16], P('adapter'), may hold values from -0.09375 to 0.09375
- up_weight: bfloat16 [16, 16, 4096], P('adapter', None, 'tensor'), may hold values from -1.5 to 1.5
- column_scale: bfloat16 [16, 4096], P('adapter', 'tensor'), may hold values from 0.5 to 2
- rotated_key_cache: bfloat16 [256, 512, 1024], P('adapter', None, 'tensor'), may hold values from -600 to 600
- cached_value_rows: bfloat16 [256, 512, 1024], P('adapter', None, 'tensor'), may hold values from -6 to 6
- cache_lengths: int32 [256], P('adapter'), may hold values from 64 to 512
Outputs:
- attention: bfloat16 [256, 4096], P('adapter', 'tensor')
Inputs may be any that keep to these rules, and one draw needn't show every extreme that they name: `request_adapter`: among the requests of one device, at most 2 use the same adapter. `adapter_table_row`: A permutation. Table row r is held by index r // 2 of the adapter axis.
All inputs are finite; a program needn't handle non-finite values.
Results may differ from a plain program's by a relative error of at most 0.022.
Values may be sent and summed in bfloat16 or wider, within the bound.
A program may use at most 64 MiB of HBM per device.

v0:
```python
import jax
import jax.numpy as jnp
from jax import lax
from jax.sharding import PartitionSpec as P

HEAD_SIZE = 128
CAP = 2


ROPE_BASE = 500000.0


def rotate(queries, lengths):
    half_size = HEAD_SIZE // 2
    frequency = ROPE_BASE ** (-(jnp.arange(half_size, dtype=jnp.float32) * 2.0) / HEAD_SIZE)
    angles = (lengths - 1).astype(jnp.float32)[:, None] * frequency[None, :]
    cosine = jnp.cos(angles)[:, None, :]
    sine_part = jnp.sin(angles)[:, None, :]
    front_half = queries[..., :half_size]
    back_half = queries[..., half_size:]
    return jnp.concatenate(
        [front_half * cosine - back_half * sine_part, back_half * cosine + front_half * sine_part],
        axis=-1,
    )


def shards(
    hidden,
    request_adapter,
    adapter_table_row,
    query_base_weight,
    down_weight,
    up_weight,
    column_scale,
    rotated_key_cache,
    cached_value_rows,
    cache_lengths,
):
    owners = lax.axis_size("adapter")
    requests_here = hidden.shape[0]
    adapter_count = down_weight.shape[0]
    columns = query_base_weight.shape[1]
    table_size = adapter_count * owners
    gathered = lax.all_gather(hidden, "tensor", axis=1, tiled=True)
    base_query = jnp.dot(gathered, query_base_weight, preferred_element_type=jnp.float32)
    lookup = (
        request_adapter[:, 0][:, None] == jnp.arange(table_size, dtype=jnp.int32)[None, :]
    ).astype(jnp.int32)
    request_table_rows = jnp.sum(lookup * adapter_table_row[None, :], axis=1)
    positions = jnp.arange(requests_here, dtype=jnp.int32)
    matching = (request_table_rows[:, None] == request_table_rows[None, :]) & (
        positions[:, None] > positions[None, :]
    )
    slot_index = request_table_rows * CAP + jnp.sum(matching.astype(jnp.int32), axis=1)
    placing = (
        jnp.arange(table_size * CAP, dtype=jnp.int32)[:, None] == slot_index[None, :]
    ).astype(jnp.bfloat16)
    outgoing_slots = jnp.dot(placing, gathered, preferred_element_type=jnp.float32).astype(
        jnp.bfloat16
    )
    outgoing_slots = outgoing_slots.reshape(owners, adapter_count, CAP, gathered.shape[1])
    partial_rank = jnp.einsum(
        "skcw,kwr->skcr",
        lax.all_to_all(outgoing_slots, "adapter", split_axis=0, concat_axis=0, tiled=True),
        down_weight,
        preferred_element_type=jnp.float32,
    )
    reduced_input = partial_rank.astype(jnp.bfloat16)
    adapter_delta = jnp.einsum(
        "epgh,phx->epgx", reduced_input, up_weight, preferred_element_type=jnp.float32
    ).astype(jnp.bfloat16)
    magnitude = jnp.broadcast_to(column_scale[None, :, None, :], adapter_delta.shape)
    slot_delta = lax.all_to_all(adapter_delta, "adapter", split_axis=0, concat_axis=0, tiled=True)
    slot_scale = lax.all_to_all(magnitude, "adapter", split_axis=0, concat_axis=0, tiled=True)
    unplacing = placing.T
    adapter_delta = jnp.dot(
        unplacing, slot_delta.reshape(table_size * CAP, columns), preferred_element_type=jnp.float32
    )
    magnitude = jnp.dot(
        unplacing, slot_scale.reshape(table_size * CAP, columns), preferred_element_type=jnp.float32
    )
    queries = (base_query + adapter_delta) * magnitude
    head_count = columns // HEAD_SIZE
    kv_count = rotated_key_cache.shape[2] // HEAD_SIZE
    group_size = head_count // kv_count
    rotated = rotate(queries.reshape(requests_here, head_count, HEAD_SIZE), cache_lengths).astype(
        jnp.bfloat16
    )
    grouped = rotated.reshape(requests_here, kv_count, group_size, HEAD_SIZE)
    context = rotated_key_cache.shape[1]
    key_rows = rotated_key_cache.reshape(requests_here, context, kv_count, HEAD_SIZE)
    value_rows = cached_value_rows.reshape(requests_here, context, kv_count, HEAD_SIZE)
    scores = jnp.einsum(
        "nkgd,ntkd->nkgt", grouped, key_rows, preferred_element_type=jnp.float32
    ) * HEAD_SIZE ** (-0.5)
    valid = (jnp.arange(context, dtype=jnp.int32)[None, :] < cache_lengths[:, None])[
        :, None, None, :
    ]
    scores = jnp.where(valid, scores, -1e30)
    highest = jnp.max(scores, axis=-1, keepdims=True)
    weights = jnp.where(valid, jnp.exp(scores - highest), 0.0)
    totals = jnp.sum(weights, axis=-1)
    rounded = weights.astype(jnp.bfloat16)
    mixed = (
        jnp.einsum("nkgt,ntkd->nkgd", rounded, value_rows, preferred_element_type=jnp.float32)
        / totals[..., None]
    )
    return mixed.astype(jnp.bfloat16).reshape(requests_here, columns)


def solution(mesh):
    in_specs = (
        P("adapter", "tensor"),
        P("adapter", None),
        P(),
        P(None, "tensor"),
        P("adapter", None, None),
        P("adapter", None, "tensor"),
        P("adapter", "tensor"),
        P("adapter", None, "tensor"),
        P("adapter", None, "tensor"),
        P("adapter"),
    )
    out_specs = P("adapter", "tensor")
    return jax.shard_map(shards, mesh=mesh, in_specs=in_specs, out_specs=out_specs, check_vma=False)
```

profile of v0, /device:TPU:0, one launch (start us, length us, event | category | flops | bytes accessed | tf_op | source)
XLA Modules:
  0.0 61.8 jit_solution(15604676640387588781)
XLA Ops:
  0.0 0.0 copy-start
  0.0 1.4 %broadcast_in_dim.17 = bf16[8,2,2,1024]{3,2,1,0:T(2,128)(2,1)} broadcast(bf16[2,1024]{1,0:T(2,128)(2,1)} %param.16), dimensions={1,3} | broadcast | bytes 69632 | tf_op jit(solution)/shard_map/broadcast_in_dim | solution.py:72
  1.4 7.3 %all-to-all-start.2 = ((bf16[8,2,2,1024]{3,2,1,0:T(2,128)(2,1)}), bf16[8,2,2,1024]{3,2,1,0:T(2,128)(2,1)S(1)}, u32[]{:S(2)}, u32[]{:S(2)}) async-start(bf16[8,2,2,1024]{3,2,1,0:T(2,128)(2,1)} %broadcast_in_dim.17), calls=%async_computation.2 | async-start | bytes 131072 | tf_op jit(solution)/shard_map/all_to_all | solution.py:74
  8.7 0.8 %select_reduce_fusion = s32[32]{0:T(128)S(1)} fusion(s32[16]{0:T(128)} %param.12, s32[32]{0:T(128)} %bitcast.57), kind=kLoop, calls=%fused_computation.43 | loop fusion | flops 1504 | bytes 320 | tf_op jit(solution)/shard_map/reduce_sum | solution.py:49
  9.5 0.2 convert_reduce_fusion
  9.7 6.0 %all_gather.3 = bf16[32,4096]{1,0:T(8,128)(2,1)S(1)} all-gather(bf16[32,1024]{1,0:T(8,128)(2,1)} %param.10), channel_id=1, replica_groups=mesh['adapter'=8,'tensor'=4] {'tensor'}, dimensions={1}, use_global_device_ids=true | all-gather | bytes 327680 | tf_op jit(solution)/shard_map/all_gather | solution.py:44
  15.6 0.2 convolution_convert_fusion
  15.9 0.9 %reshape.107 = bf16[8,2,2,4096]{3,2,1,0:T(2,128)(2,1)} reshape(bf16[32,4096]{1,0:T(8,128)(2,1)S(1)} %convolution_convert_fusion) | data formatting | bytes 524288 | tf_op jit(solution)/shard_map/reshape | solution.py:61
  16.7 0.7 %add_convert_fusion.1 = f32[32]{0:T(128)S(1)} fusion(s32[32]{0:T(128)} %param.19), kind=kLoop, calls=%fused_computation.46 | loop fusion | flops 64 | bytes 256 | tf_op jit(solution)/shard_map/convert_element_type | solution.py:16
  17.4 0.0 all-to-all-done.2
  17.4 6.0 %all-to-all-start = ((bf16[8,2,2,4096]{3,2,1,0:T(2,128)(2,1)}), bf16[8,2,2,4096]{3,2,1,0:T(2,128)(2,1)S(1)}, u32[]{:S(2)}, u32[]{:S(2)}) async-start(bf16[8,2,2,4096]{3,2,1,0:T(2,128)(2,1)} %reshape.107), calls=%async_computation | async-start | bytes 524288 | tf_op jit(solution)/shard_map/all_to_all | solution.py:64
  23.4 0.7 %iota_compare_fusion = pred[32,512]{1,0:T(8,128)(4,1)S(1)} fusion(s32[32]{0:T(128)} %param.19), kind=kLoop, calls=%fused_computation.31 | loop fusion | flops 16384 | bytes 16512 | tf_op jit(solution)/shard_map/lt | solution.py:96
  24.2 0.1 multiply_cosine_fusion
  24.3 8.5 %all-to-all-done = bf16[8,2,2,4096]{3,2,1,0:T(2,128)(2,1)S(1)} async-done(((bf16[8,2,2,4096]{3,2,1,0:T(2,128)(2,1)}), bf16[8,2,2,4096]{3,2,1,0:T(2,128)(2,1)S(1)}, u32[]{:S(2)}, u32[]{:S(2)}) %all-to-all-start) | async-done | bytes 262176 | tf_op jit(solution)/shard_map/all_to_all | solution.py:64
  32.8 0.0 copy-done
  32.8 1.3 %fusion.15 = bf16[8,2,2,1024]{3,0,2,1:T(8,128)(2,1)S(1)} fusion(bf16[2,4096,16]{1,2,0:T(8,128)(2,1)S(1)} %copy-done, bf16[8,2,2,4096]{3,2,1,0:T(2,128)(2,1)S(1)} %all-to-all-done, bf16[2,16,1024]{2,1,0:T(8,128)(2,1)} %param.15), kind=kOutput, calls=%fused_computation.16 | convolution fusion | flops 5276160 | bytes 655360 | tf_op jit(solution)/shard_map/epgh,phx->epgx/dot_general | solution.py:69
  34.1 0.7 %copy.25 = bf16[8,2,2,1024]{3,2,1,0:T(2,128)(2,1)} copy(bf16[8,2,2,1024]{3,0,2,1:T(8,128)(2,1)S(1)} %fusion.15) | data formatting | bytes 131072 | tf_op jit(solution)/shard_map/convert_element_type | solution.py:71
  34.8 3.6 %all-to-all-start.1 = ((bf16[8,2,2,1024]{3,2,1,0:T(2,128)(2,1)}), bf16[8,2,2,1024]{3,2,1,0:T(2,128)(2,1)S(1)}, u32[]{:S(2)}, u32[]{:S(2)}) async-start(bf16[8,2,2,1024]{3,2,1,0:T(2,128)(2,1)} %copy.25), calls=%async_computation.1 | async-start | bytes 131072 | tf_op jit(solution)/shard_map/all_to_all | solution.py:73
  38.4 0.2 fusion.35
  38.6 6.7 %all-to-all-done.1 = bf16[8,2,2,1024]{3,2,1,0:T(2,128)(2,1)S(1)} async-done(((bf16[8,2,2,1024]{3,2,1,0:T(2,128)(2,1)}), bf16[8,2,2,1024]{3,2,1,0:T(2,128)(2,1)S(1)}, u32[]{:S(2)}, u32[]{:S(2)}) %all-to-all-start.1) | async-done | bytes 65568 | tf_op jit(solution)/shard_map/all_to_all | solution.py:73
  45.3 0.2 fusion.36
  45.5 4.9 %fusion.14 = f32[4,8,8,128]{3,1,2,0:T(8,128)S(1)} fusion(f32[32,1024]{1,0:T(8,128)S(1)} %fusion.35, f32[32,1024]{1,0:T(8,128)S(1)} %fusion.36, bf16[32,4096]{1,0:T(8,128)(2,1)S(1)} %all_gather.3, bf16[4096,1024]{1,0:T(8,128)(2,1)} %param.13), kind=kOutput, calls=%fused_computation.14 | convolution fusion | flops 268500992 | bytes 9043968 | tf_op jit(solution)/shard_map/dot_general | solution.py:45
  50.5 0.1 subtract_convert_fusion
  50.6 5.9 %fusion.42 = (f32[32,2,4]{2,1,0:T(2,128)S(1)}, bf16[32,2,4,512]{3,2,1,0:T(4,128)(2,1)S(1)}) fusion(pred[32,512]{1,0:T(8,128)(4,1)S(1)} %iota_compare_fusion, bf16[32,2,4,64]{3,2,1,0:T(4,128)(2,1)S(1)} %bitcast.56, bf16[32,2,4,64]{3,2,1,0:T(4,128)(2,1)S(1)} %bitcast.55, bf16[32,512,256]{2,1,0:T(8,128)(2,1)} %param.17), kind=kOutput, calls=%fused_computation.49 | convolution fusion | flops 34472448 | bytes 8733696 | tf_op jit(solution)/shard_map/sub | solution.py:101
  56.5 4.6 %fusion.23 = bf16[32,2,4,128]{3,2,1,0:T(4,128)(2,1)S(1)} fusion(bf16[32,2,4,512]{3,2,1,0:T(4,128)(2,1)S(1)} %get-tuple-element.10, f32[32,2,4]{2,1,0:T(2,128)S(1)} %get-tuple-element.9, bf16[32,512,256]{2,1,0:T(8,128)(2,1)} %param.18), kind=kOutput, calls=%fused_computation.21 | convolution fusion | flops 33619968 | bytes 8717312 | tf_op jit(solution)/shard_map/nkgt,ntkd->nkgd/dot_general | solution.py:105
  61.1 0.7 %reshape.113 = bf16[32,1024]{1,0:T(8,128)(2,1)} reshape(bf16[32,2,4,128]{3,2,1,0:T(4,128)(2,1)S(1)} %fusion.23) | data formatting | bytes 131072 | tf_op jit(solution)/shard_map/reshape | solution.py:108
  (5 shorter events, 0.1 us)
Async XLA Ops:
  0.0 32.8 %copy-start = (bf16[2,4096,16]{1,2,0:T(8,128)(2,1)S(1)}, bf16[2,4096,16]{1,2,0:T(8,128)(2,1)}, u32[]{:S(2)}) copy-start(bf16[2,4096,16]{1,2,0:T(8,128)(2,1)} %param.14) | copy-start | bytes 786436
  1.4 16.0 %all-to-all-start.2 = ((bf16[8,2,2,1024]{3,2,1,0:T(2,128)(2,1)}), bf16[8,2,2,1024]{3,2,1,0:T(2,128)(2,1)S(1)}, u32[]{:S(2)}, u32[]{:S(2)}) async-start(bf16[8,2,2,1024]{3,2,1,0:T(2,128)(2,1)} %broadcast_in_dim.17), calls=%async_computation.2 | async-start | bytes 131072 | tf_op jit(solution)/shard_map/all_to_all | solution.py:74
  17.4 15.4 %all-to-all-start = ((bf16[8,2,2,4096]{3,2,1,0:T(2,128)(2,1)}), bf16[8,2,2,4096]{3,2,1,0:T(2,128)(2,1)S(1)}, u32[]{:S(2)}, u32[]{:S(2)}) async-start(bf16[8,2,2,4096]{3,2,1,0:T(2,128)(2,1)} %reshape.107), calls=%async_computation | async-start | bytes 524288 | tf_op jit(solution)/shard_map/all_to_all | solution.py:64
  34.8 10.5 %all-to-all-start.1 = ((bf16[8,2,2,1024]{3,2,1,0:T(2,128)(2,1)}), bf16[8,2,2,1024]{3,2,1,0:T(2,128)(2,1)S(1)}, u32[]{:S(2)}, u32[]{:S(2)}) async-start(bf16[8,2,2,1024]{3,2,1,0:T(2,128)(2,1)} %copy.25), calls=%async_computation.1 | async-start | bytes 131072 | tf_op jit(solution)/shard_map/all_to_all | solution.py:73
where the time goes:
time: 62.3 us; the launch traced here: 61.8 us
  matrix products  17.3 us (28%)
  starting transfers between devices  16.9 us (27%)
  waiting for transfers between devices  15.2 us (24%)
  blocking collectives  5.99 us (10%)
  local copies, waits for them, and re-layouts  3.76 us (6%)
  other arithmetic  2.6 us (4%)
    all_to_all x1, waiting for transfers between devices, shards(): lax.all_to_all(outgoing_slots, 'adapter', split_axis=0, concat_axis=0, ti...  8.5 us
    all_to_all x1, starting transfers between devices, shards(): lax.all_to_all(magnitude, 'adapter', split_axis=0, concat_axis=0, tiled=T...  7.31 us
    all_to_all x1, waiting for transfers between devices, shards(): lax.all_to_all(adapter_delta, 'adapter', split_axis=0, concat_axis=0, til...  6.7 us
    all_to_all x1, starting transfers between devices, shards(): lax.all_to_all(outgoing_slots, 'adapter', split_axis=0, concat_axis=0, ti...  6 us
    all_gather x1, blocking collectives, shards(): gathered = lax.all_gather(hidden, 'tensor', axis=1, tiled=True)  5.99 us
    sub x1, matrix products, shards(): weights = jnp.where(valid, jnp.exp(scores - highest), 0.0)  5.88 us
    dot_general x1, matrix products, shards(): jnp.dot(gathered, query_base_weight, preferred_element_type=jnp.float32)  4.94 us
    dot_general x1, matrix products, shards(): jnp.einsum('nkgt,ntkd->nkgd', rounded, value_rows, preferred_element_type...  4.57 us
  transfers between devices with their start and end apart: 3, of which 2 were waited for; matrix products, arithmetic and copies ran while one was open for 6% of the time, Pallas kernels for 0%

commit v1 on v0

v1 whole, which is shorter than its diff:
```python
import functools
import math

import jax
import jax.numpy as jnp
from jax import lax
from jax.experimental import pallas as pl
from jax.experimental.pallas import tpu as pltpu
from jax.sharding import PartitionSpec as P

HEAD_SIZE = 128
CAP = 2
ROPE_BASE = 500000.0
BLOCK_ROWS = 16
GROUP = 8
MESH = pl.DeviceIdType.MESH
LAST = (((1,), (1,)), ((), ()))
F32 = jnp.float32
BF16 = jnp.bfloat16


def iota(shape, dim):
    return lax.broadcasted_iota(jnp.int32, shape, dim)


def kernel(
    owners,
    parts,
    chunks_kv,
    hidden,
    request_adapter,
    table,
    weight,
    down,
    up,
    scale,
    keys,
    values,
    lengths,
    out,
    hid_all,
    w_v,
    down_v,
    up_v,
    scale_v,
    k_v,
    v_v,
    slot_out,
    slot_in,
    scale_out,
    scale_in,
    delta_out,
    delta_in,
    rank_out,
    rank_in,
    q_rows,
    att,
    small_sem,
    w_sem,
    k_sem,
    v_sem,
    slot_send,
    slot_recv,
    scale_send,
    scale_recv,
    delta_send,
    delta_recv,
    hid_send,
    hid_recv,
    rank_send,
    rank_recv,
):
    a = lax.axis_index("adapter")
    t = lax.axis_index("tensor")
    barrier = pltpu.get_barrier_semaphore()
    for d in range(1, owners):
        pl.semaphore_signal(
            barrier, inc=1, device_id=(lax.rem(a + d, owners), t), device_id_type=MESH
        )
    for d in range(1, parts):
        pl.semaphore_signal(
            barrier, inc=1, device_id=(a, lax.rem(t + d, parts)), device_id_type=MESH
        )

    n, feats = hidden.shape
    adapters, rank, columns = up.shape
    slots = adapters * CAP
    chunks = BLOCK_ROWS // slots
    wide_in = feats // chunks
    wide_out = columns // chunks
    lanes = owners * BLOCK_ROWS
    context, kv_width = keys.shape[1], keys.shape[2]
    kv_count = kv_width // HEAD_SIZE
    heads = columns // HEAD_SIZE
    per_kv = heads // kv_count
    row_pad = q_rows.shape[1] // n

    def local(src, dst, sem):
        copy = pltpu.make_async_copy(src, dst, sem)
        copy.start()
        return copy

    hid_copy = local(hidden, hid_all.at[t], small_sem.at[0])
    scale_copy = local(scale, scale_v, small_sem.at[1])
    down_copy = local(
        down.at[:, :, pl.ds(pl.multiple_of(t * feats, 128), feats)], down_v, small_sem.at[2]
    )
    up_copy = local(up, up_v, small_sem.at[3])
    order = [lax.rem(t + d, parts) for d in range(parts)]
    w_copies = [
        local(
            weight.at[pl.ds(pl.multiple_of(order[d] * feats, 128), feats), :],
            w_v.at[d],
            w_sem.at[d],
        )
        for d in range(parts)
    ]
    step = n // chunks_kv
    k_copies = [
        local(keys.at[pl.ds(i * step, step)], k_v.at[pl.ds(i * step, step)], k_sem.at[i])
        for i in range(chunks_kv)
    ]
    v_copies = [
        local(values.at[pl.ds(i * step, step)], v_v.at[pl.ds(i * step, step)], v_sem.at[i])
        for i in range(chunks_kv)
    ]

    side = chunks * n
    rows_n = iota((n, 128), 0)
    row_of = jnp.zeros((n, 128), F32)
    length_of = jnp.zeros((n, 128), F32)
    for i in range(n):
        here = rows_n == i
        row_of = jnp.where(here, table[request_adapter[i]].astype(F32), row_of)
        length_of = jnp.where(here, lengths[i].astype(F32), length_of)
    row_sq = jnp.concatenate([row_of] * chunks, axis=0)
    row_sq_t = jnp.transpose(row_sq)
    r_i = iota((side, side), 0)
    l_i = iota((side, side), 1)
    earlier = (row_sq == row_sq_t) & (l_i < r_i % n)
    repeat = jnp.sum(jnp.where(earlier, 1.0, 0.0), axis=1, keepdims=True)
    slot_col = (row_sq[:, :1] * CAP + repeat).astype(jnp.int32)
    r_i = iota((side, lanes), 0)
    l_i = iota((side, lanes), 1)
    take = (slot_col == (l_i // BLOCK_ROWS) * slots + l_i % slots) & (
        (l_i // slots) % chunks == r_i // n
    )
    unplace = jnp.where(take, 1.0, 0.0)
    place = jnp.transpose(unplace).astype(BF16)
    unplace = unplace.astype(BF16)

    hid_copy.wait()
    own = hid_all[t]
    stacked = jnp.concatenate(
        [own[:, c * wide_in : (c + 1) * wide_in] for c in range(chunks)], axis=0
    )
    slot_out[...] = (
        jnp.dot(place, stacked, preferred_element_type=F32)
        .astype(BF16)
        .reshape(owners, BLOCK_ROWS, wide_in)
    )
    slot_in[a] = slot_out[a]

    pl.semaphore_wait(barrier, owners - 1 + parts - 1)

    def across(d, src, dst, send, recv):
        copy = pltpu.make_async_remote_copy(
            src_ref=src,
            dst_ref=dst,
            send_sem=send.at[d],
            recv_sem=recv.at[d],
            device_id=(lax.rem(a + d, owners), t),
            device_id_type=MESH,
        )
        copy.start()
        return copy

    def beside(d, src, dst, send, recv):
        copy = pltpu.make_async_remote_copy(
            src_ref=src,
            dst_ref=dst,
            send_sem=send.at[d],
            recv_sem=recv.at[d],
            device_id=(a, lax.rem(t + d, parts)),
            device_id_type=MESH,
        )
        copy.start()
        return copy

    slot_copies = [
        across(d, slot_out.at[lax.rem(a + d, owners)], slot_in.at[a], slot_send, slot_recv)
        for d in range(1, owners)
    ]
    hid_copies = [
        beside(d, hid_all.at[t], hid_all.at[t], hid_send, hid_recv) for d in range(1, parts)
    ]

    scale_copy.wait()
    block_row = iota((BLOCK_ROWS, wide_out), 0)
    block = jnp.zeros((BLOCK_ROWS, wide_out), F32)
    scale_f = scale_v[...].astype(F32)
    for c in range(chunks):
        for k in range(adapters):
            piece = scale_f[k : k + 1, c * wide_out : (c + 1) * wide_out]
            at = (block_row // slots == c) & ((block_row % slots) // CAP == k)
            block = jnp.where(at, piece, block)
    scale_out[...] = block.astype(BF16)
    scale_in[a] = scale_out[...]
    scale_copies = [
        across(d, scale_out, scale_in.at[a], scale_send, scale_recv) for d in range(1, owners)
    ]

    lane = iota((n, HEAD_SIZE), 1)
    half = HEAD_SIZE // 2
    frequency = jnp.exp((lane % half).astype(F32) * (-2.0 * math.log(ROPE_BASE) / HEAD_SIZE))
    angles = (length_of - 1.0) * frequency
    cosine = jnp.cos(angles)
    sine = jnp.sin(angles) * jnp.where(lane < half, -1.0, 1.0)
    q_rows[...] = jnp.zeros_like(q_rows)

    def base_part(d, block):
        w_copies[d].wait()
        return jnp.dot(block, w_v[d], preferred_element_type=F32)

    base = base_part(0, own)

    def received(d, copies):
        copies[d - 1].wait_recv()

    m_r = iota((chunks * adapters * rank, lanes), 0)
    m_l = iota((chunks * adapters * rank, lanes), 1)
    mask = (m_r // (adapters * rank) == (m_l // slots) % chunks) & (
        (m_r // rank) % adapters == (m_l % slots) // CAP
    )
    down_copy.wait()
    down_rows = down_v[...].reshape(adapters * rank, feats)
    down_rows = jnp.concatenate(
        [down_rows[:, c * wide_in : (c + 1) * wide_in] for c in range(chunks)], axis=0
    )
    for d in range(1, owners):
        received(d, slot_copies)
    arrived = slot_in[...].reshape(lanes, wide_in)
    products = lax.dot_general(down_rows, arrived, LAST, preferred_element_type=F32)
    products = jnp.where(mask, products, 0.0)
    partial = products[:rank]
    for i in range(1, chunks * adapters):
        partial = partial + products[i * rank : (i + 1) * rank]
    rank_out[...] = partial
    rank_copies = [
        beside(d, rank_out, rank_in.at[t], rank_send, rank_recv) for d in range(1, parts)
    ]
    rank_in[t] = partial

    half_parts = 1 + (parts - 1) // 2
    for d in range(1, half_parts):
        received(d, hid_copies)
        base = base + base_part(parts - d, hid_all[lax.rem(t + parts - d, parts)])

    up_copy.wait()
    up_rows = up_v[...].reshape(adapters * rank, columns)
    up_rows = jnp.concatenate(
        [up_rows[:, c * wide_out : (c + 1) * wide_out] for c in range(chunks)], axis=0
    )
    for d in range(1, parts):
        received(d, rank_copies)
    total = rank_in[0]
    for i in range(1, parts):
        total = total + rank_in[i]
    chunk_of = (iota((rank, lanes), 1) // slots) % chunks
    hop = 1
    while hop < chunks:
        shift = hop * slots
        total = total + jnp.where(
            (chunk_of // hop) % 2 == 0,
            pltpu.roll(total, lanes - shift, 1),
            pltpu.roll(total, shift, 1),
        )
        hop *= 2
    spread = jnp.where(mask, jnp.concatenate([total] * (chunks * adapters), axis=0), 0.0)
    spread = jnp.transpose(spread).astype(BF16)
    delta_out[...] = (
        jnp.dot(spread, up_rows, preferred_element_type=F32)
        .astype(BF16)
        .reshape(owners, BLOCK_ROWS, wide_out)
    )
    delta_copies = [
        across(d, delta_out.at[lax.rem(a + d, owners)], delta_in.at[a], delta_send, delta_recv)
        for d in range(1, owners)
    ]
    delta_in[a] = delta_out[a]

    for d in range(half_parts, parts):
        received(d, hid_copies)
        base = base + base_part(parts - d, hid_all[lax.rem(t + parts - d, parts)])
    for d in range(1, owners):
        received(d, scale_copies)
    magnitude = jnp.dot(
        unplace, scale_in[...].reshape(lanes, wide_out), preferred_element_type=F32
    )
    for copy in k_copies + v_copies:
        copy.wait()
    for d in range(1, owners):
        received(d, delta_copies)
    delta = jnp.dot(unplace, delta_in[...].reshape(lanes, wide_out), preferred_element_type=F32)

    for h in range(heads):
        c, at = divmod(h * HEAD_SIZE, wide_out)
        cut = slice(at, at + HEAD_SIZE)
        query = (
            base[:, h * HEAD_SIZE : (h + 1) * HEAD_SIZE] + delta[c * n : (c + 1) * n, cut]
        ) * magnitude[c * n : (c + 1) * n, cut]
        rotated = query * cosine + pltpu.roll(query, half, 1) * sine
        kv = h // per_kv
        q_rows[kv, pl.ds(h, n, stride=row_pad), :] = rotated

    slot_of = iota((row_pad, context), 1)
    head_row = iota((row_pad, HEAD_SIZE), 0)

    def attend(g, _):
        first = g * GROUP
        scores = []
        for i in range(GROUP):
            at = pl.multiple_of((first + i) * row_pad, 8)
            q = jnp.concatenate(
                [q_rows[kv, pl.ds(at, row_pad), :] for kv in range(kv_count)], axis=1
            ).astype(BF16)
            scores.append(
                lax.dot_general(q, k_v[first + i], LAST, preferred_element_type=F32)
            )
        weights, totals = [], []
        for i in range(GROUP):
            s = jnp.where(slot_of < lengths[first + i], scores[i], -1e30)
            highest = jnp.max(s, axis=1, keepdims=True)
            w = jnp.exp((s - highest) * HEAD_SIZE ** (-0.5))
            totals.append(jnp.sum(w, axis=1, keepdims=True))
            weights.append(w.astype(BF16))
        for i in range(GROUP):
            mixed = jnp.dot(weights[i], v_v[first + i], preferred_element_type=F32)
            picked = mixed[:, :HEAD_SIZE]
            for kv in range(1, kv_count):
                picked = jnp.where(
                    head_row >= kv * per_kv,
                    mixed[:, kv * HEAD_SIZE : (kv + 1) * HEAD_SIZE],
                    picked,
                )
            at = pl.multiple_of((first + i) * row_pad, 8)
            att[pl.ds(at, row_pad), :] = picked / totals[i]
        return 0

    lax.fori_loop(0, n // GROUP, attend, 0)
    for h in range(heads):
        out[:, h * HEAD_SIZE : (h + 1) * HEAD_SIZE] = att[
            pl.ds(h, n, stride=row_pad), :
        ].astype(BF16)
    for copy in slot_copies + scale_copies + delta_copies + hid_copies + rank_copies:
        copy.wait_send()


def shards(
    hidden,
    request_adapter,
    adapter_table_row,
    query_base_weight,
    down_weight,
    up_weight,
    column_scale,
    rotated_key_cache,
    cached_value_rows,
    cache_lengths,
):
    owners = lax.axis_size("adapter")
    parts = lax.axis_size("tensor")
    n, feats = hidden.shape
    adapters, rank, columns = up_weight.shape
    chunks = BLOCK_ROWS // (adapters * CAP)
    lanes = owners * BLOCK_ROWS
    heads = columns // HEAD_SIZE
    row_pad = -(-heads // 8) * 8
    context, kv_width = rotated_key_cache.shape[1:]
    wide_in, wide_out = feats // chunks, columns // chunks
    chunks_kv = 4
    anywhere = pl.BlockSpec(memory_space=pl.ANY)
    scalars = pl.BlockSpec(memory_space=pltpu.SMEM)
    dma = pltpu.SemaphoreType.DMA
    return pl.pallas_call(
        functools.partial(kernel, owners, parts, chunks_kv),
        out_shape=jax.ShapeDtypeStruct((n, columns), BF16),
        in_specs=[anywhere, scalars, scalars] + [anywhere] * 6 + [scalars],
        out_specs=pl.BlockSpec(memory_space=pltpu.VMEM),
        scratch_shapes=[
            pltpu.VMEM((parts, n, feats), BF16),
            pltpu.VMEM((parts, feats, columns), BF16),
            pltpu.VMEM((adapters, rank, feats), BF16),
            pltpu.VMEM((adapters, rank, columns), BF16),
            pltpu.VMEM((adapters, columns), BF16),
            pltpu.VMEM((n, context, kv_width), BF16),
            pltpu.VMEM((n, context, kv_width), BF16),
            pltpu.VMEM((owners, BLOCK_ROWS, wide_in), BF16),
            pltpu.VMEM((owners, BLOCK_ROWS, wide_in), BF16),
            pltpu.VMEM((BLOCK_ROWS, wide_out), BF16),
            pltpu.VMEM((owners, BLOCK_ROWS, wide_out), BF16),
            pltpu.VMEM((owners, BLOCK_ROWS, wide_out), BF16),
            pltpu.VMEM((owners, BLOCK_ROWS, wide_out), BF16),
            pltpu.VMEM((rank, lanes), F32),
            pltpu.VMEM((parts, rank, lanes), F32),
            pltpu.VMEM((kv_width // HEAD_SIZE, n * row_pad, HEAD_SIZE), F32),
            pltpu.VMEM((n * row_pad, HEAD_SIZE), F32),
            dma((4,)),
            dma((parts,)),
            dma((chunks_kv,)),
            dma((chunks_kv,)),
        ]
        + [dma((owners,))] * 6
        + [dma((parts,))] * 4,
        compiler_params=pltpu.CompilerParams(
            collective_id=0, has_side_effects=True, vmem_limit_bytes=60 * 1024 * 1024
        ),
    )(
        hidden,
        request_adapter.reshape(n),
        adapter_table_row,
        query_base_weight,
        jnp.swapaxes(down_weight, 1, 2),
        up_weight,
        column_scale,
        rotated_key_cache,
        cached_value_rows,
        cache_lengths,
    )


def solution(mesh):
    in_specs = (
        P("adapter", "tensor"),
        P("adapter", None),
        P(),
        P(None, "tensor"),
        P("adapter", None, None),
        P("adapter", None, "tensor"),
        P("adapter", "tensor"),
        P("adapter", None, "tensor"),
        P("adapter", None, "tensor"),
        P("adapter"),
    )
    out_specs = P("adapter", "tensor")
    return jax.shard_map(shards, mesh=mesh, in_specs=in_specs, out_specs=out_specs, check_vma=False)
```

time: 62.3 us -> 25.8 us (0.41)
  Pallas kernels: 0 us -> 24.2 us
  matrix products: 17.3 us -> 0 us
  starting transfers between devices: 16.9 us -> 0 us
  waiting for transfers between devices: 15.2 us -> 0 us
  blocking collectives: 5.99 us -> 0 us
  other arithmetic: 2.6 us -> 0 us
  local copies, waits for them, and re-layouts: 3.76 us -> 1.47 us
    pallas_call x0 -> x1, Pallas kernels: none -> 24.2 us  [shards(): pl.pallas_call(functools.partial(kernel, owners, parts, chunks_kv), out_s...]
    all_to_all x3 -> x0, starting transfers between devices: 16.9 us -> none  [the longest x1 7.31 us: shards(): lax.all_to_all(magnitude, 'adapter', split_axis=0, concat_axis=0, tiled=T...]
    all_to_all x3 -> x0, waiting for transfers between devices: 15.2 us -> none  [the longest x1 8.5 us: shards(): lax.all_to_all(outgoing_slots, 'adapter', split_axis=0, concat_axis=0, ti...]
    dot_general x6 -> x0, matrix products: 11.4 us -> none  [the longest x1 4.94 us: shards(): jnp.dot(gathered, query_base_weight, preferred_element_type=jnp.float32)]
    all_gather x1 -> x0, blocking collectives: 5.99 us -> none  [shards(): gathered = lax.all_gather(hidden, 'tensor', axis=1, tiled=True)]
    sub x1 -> x0, matrix products: 5.88 us -> none  [shards(): weights = jnp.where(valid, jnp.exp(scores - highest), 0.0)]
    reshape x4 -> x0, local copies, waits for them, and re-layouts: 1.63 us -> none  [the longest x1 0.89 us: shards(): outgoing_slots.reshape(owners, adapter_count, CAP, gathered.shape[1])]
    unnamed x3 -> x1, local copies, waits for them, and re-layouts: 0.03 us -> 1.47 us
  transfers between devices with their start and end apart: 3 -> 0, of which waited for: 2 -> 0; matrix products, arithmetic and copies ran while one was open for 6% -> 0% of each run, Pallas kernels for 0% -> 0%
where the time goes in v1:
time: 25.8 us; the launch traced here: 25.7 us
  Pallas kernels  24.2 us (94%)
  local copies, waits for them, and re-layouts  1.47 us (6%)
    pallas_call x1, Pallas kernels, shards(): pl.pallas_call(functools.partial(kernel, owners, parts, chunks_kv), out_s...  24.2 us
    unnamed x1, local copies, waits for them, and re-layouts  1.47 us

profile of v1, /device:TPU:0, one launch (start us, length us, event | category | flops | bytes accessed | tf_op | source)
XLA Modules:
  0.0 25.7 jit_solution(10123747246502988581)
XLA Ops:
  0.0 24.2 %shard_map.100 = bf16[32,1024]{1,0:T(8,128)(2,1)} custom-call(bf16[32,1024]{1,0:T(8,128)(2,1)} %hidden.1, s32[32]{0:T(128)} %bitcast.3, s32[16]{0:T(128)} %table.1, bf16[4096,1024]{1,0:T(8,128)(2,1)} %weight.1, bf16[2,16,4096]{2,1,0:T(8,128)(2,1)} %bitcast.2, bf16[2,16,1024]{2,1,0:T(8,128)(2,1)} %up.1, bf16[2,1024]{1,0:T(2,128)(2,1)} %scale.1, ...), custom_call_target="tpu_custom_call" | custom-call | tf_op jit(solution)/shard_map/pallas_call | solution.py:385
  24.2 1.5 %copy.12 = bf16[32,1024]{1,0:T(8,128)(2,1)} copy(bf16[32,1024]{1,0:T(8,128)(2,1)} %shard_map.100) | data formatting | bytes 131072

commit v2 on v1

--- a/solution.py
+++ b/solution.py
@@ -206,9 +206,6 @@
             block = jnp.where(at, piece, block)
     scale_out[...] = block.astype(BF16)
     scale_in[a] = scale_out[...]
-    scale_copies = [
-        across(d, scale_out, scale_in.at[a], scale_send, scale_recv) for d in range(1, owners)
-    ]
 
     lane = iota((n, HEAD_SIZE), 1)
     half = HEAD_SIZE // 2
@@ -248,6 +245,9 @@
     rank_out[...] = partial
     rank_copies = [
         beside(d, rank_out, rank_in.at[t], rank_send, rank_recv) for d in range(1, parts)
+    ]
+    scale_copies = [
+        across(d, scale_out, scale_in.at[a], scale_send, scale_recv) for d in range(1, owners)
     ]
     rank_in[t] = partial
 
@@ -347,7 +347,8 @@
             att[pl.ds(at, row_pad), :] = picked / totals[i]
         return 0
 
-    lax.fori_loop(0, n // GROUP, attend, 0)
+    for g in range(n // GROUP):
+        attend(g, 0)
     for h in range(heads):
         out[:, h * HEAD_SIZE : (h + 1) * HEAD_SIZE] = att[
             pl.ds(h, n, stride=row_pad), :
@@ -384,7 +385,7 @@
     dma = pltpu.SemaphoreType.DMA
     return pl.pallas_call(
         functools.partial(kernel, owners, parts, chunks_kv),
-        out_shape=jax.ShapeDtypeStruct((n, columns), BF16),
+        out_shape=pltpu.VMEM((n, columns), BF16),
         in_specs=[anywhere, scalars, scalars] + [anywhere] * 6 + [scalars],
         out_specs=pl.BlockSpec(memory_space=pltpu.VMEM),
         scratch_shapes=[

time: 25.8 us -> 24 us (0.930)
  Pallas kernels: 24.2 us -> 23.2 us
  local copies, waits for them, and re-layouts: 1.47 us -> 0.63 us
    pallas_call x1, Pallas kernels: 24.2 us -> 23.2 us  [shards(): pl.pallas_call(functools.partial(kernel, owners, parts, chunks_kv), out_s...]
    unnamed x1, local copies, waits for them, and re-layouts: 1.47 us -> 0.63 us
where the time goes in v2:
time: 24 us; the launch traced here: 23.8 us
  Pallas kernels  23.2 us (97%)
  local copies, waits for them, and re-layouts  0.63 us (3%)
    pallas_call x1, Pallas kernels, shards(): pl.pallas_call(functools.partial(kernel, owners, parts, chunks_kv), out_s...  23.2 us
    unnamed x1, local copies, waits for them, and re-layouts  0.63 us

profile of v2, /device:TPU:0, one launch (start us, length us, event | category | flops | bytes accessed | tf_op | source)
XLA Modules:
  0.0 23.8 jit_solution(3410763869512663766)
XLA Ops:
  0.0 23.2 %shard_map.100 = bf16[32,1024]{1,0:T(8,128)(2,1)S(1)} custom-call(bf16[32,1024]{1,0:T(8,128)(2,1)} %hidden.1, s32[32]{0:T(128)} %bitcast.3, s32[16]{0:T(128)} %table.1, bf16[4096,1024]{1,0:T(8,128)(2,1)} %weight.1, bf16[2,16,4096]{2,1,0:T(8,128)(2,1)} %bitcast.2, bf16[2,16,1024]{2,1,0:T(8,128)(2,1)} %up.1, bf16[2,1024]{1,0:T(2,128)(2,1)} %scale.1, ...), custom_call_target="tpu_custom_call" | custom-call | tf_op jit(solution)/shard_map/pallas_call | solution.py:386
  23.2 0.6 %copy.12 = bf16[32,1024]{1,0:T(8,128)(2,1)} copy(bf16[32,1024]{1,0:T(8,128)(2,1)S(1)} %shard_map.100) | data formatting | bytes 131072
